TPU v7x, 32 devices: a whole 2x2x4 slice. The times are simulated.
32 devices in a mesh: tm: 2 (over core), space: 16 (over z, y, x).
Axes of the slice: x: 2, y: 2, z: 4, core: 2. Of those that a mesh axis runs over, the one named last changes fastest.
Arguments:
- fine: bfloat16 [8, 64, 256, 256], P('tm', 'space'), may hold values from -6 to 6
- coarse: bfloat16 [8, 32, 128, 256], P('tm', 'space'), may hold values from -6 to 6
- w_query: bfloat16 [256, 256], replicated, may hold values from -24 to 24
- w_key: bfloat16 [256, 256], replicated, may hold values from -0.375 to 0.375
- w_value: bfloat16 [256, 256], replicated, may hold values from -0.375 to 0.375
- w_out: bfloat16 [256, 256], replicated, may hold values from -0.375 to 0.375
- conv_first: bfloat16 [3, 3, 256, 256], replicated, may hold values from -0.125 to 0.125
- conv_second: bfloat16 [3, 3, 256, 256], replicated, may hold values from -0.125 to 0.125
Outputs:
- joined: bfloat16 [8, 64, 256, 256], P('tm', 'space')
All inputs are finite; a program needn't handle non-finite values.
Results may differ from a plain program's by a relative error of at most 0.009.
Values may be sent and summed in bfloat16 or wider, within the bound.
A program may use at most 128 MiB of HBM per device.

v0:
```python
import functools

import jax
import jax.numpy as jnp
from jax import lax
from jax.experimental import pallas as pl
from jax.experimental.pallas import tpu as pltpu
from jax.sharding import PartitionSpec as P

HEADS = 8
CHUNKS = 4
TILE = 64
LOG2E = 1.4426950408889634


def encode(frame_ids, width):
    half = width // 2
    index = jnp.arange(half, dtype=jnp.float32)
    inverse = jnp.exp(-jnp.log(10000.0) * 2.0 * index / width)
    angles = frame_ids.astype(jnp.float32)[:, None] * inverse[None, :]
    return jnp.concatenate([jnp.sin(angles), jnp.cos(angles)], axis=1)


def motion_kernel(mine_ref, other_ref, pos_ref, wq_ref, wkv_ref, wo_ref, out_ref):
    own, _, tile, width = mine_ref.shape
    others = other_ref.shape[0]
    depth = width // HEADS
    scale = LOG2E / (float(depth) ** 0.5)
    normed = []
    for frame in range(own + others):
        if frame < own:
            x = mine_ref[frame, 0]
        else:
            x = other_ref[frame - own, 0]
        hidden = x.astype(jnp.float32) + pos_ref[frame : frame + 1, :]
        center = hidden - jnp.mean(hidden, axis=-1, keepdims=True)
        spread = jnp.mean(center * center, axis=-1, keepdims=True)
        normed.append((center * lax.rsqrt(spread + 1e-05)).astype(jnp.bfloat16))
    flat = jnp.concatenate(normed, axis=0)
    query = jnp.dot(flat[: own * tile], wq_ref[...], preferred_element_type=jnp.float32)
    query = query.astype(jnp.bfloat16).reshape(own, tile, width)
    both = jnp.dot(flat, wkv_ref[...], preferred_element_type=jnp.float32).astype(jnp.bfloat16)
    key, value = both[:, :width], both[:, width:]
    rows = lax.broadcasted_iota(jnp.int32, (width, width), 0) // depth
    cols = lax.broadcasted_iota(jnp.int32, (width, width), 1) // depth
    blocks = jnp.where(rows == cols, 1.0, 0.0).astype(jnp.bfloat16)
    scores = []
    for other in range(own + others):
        product = query * key[other * tile : (other + 1) * tile][None]
        scores.append(jnp.dot(product.reshape(own * tile, width), blocks, preferred_element_type=jnp.float32))
    largest = functools.reduce(jnp.maximum, scores)
    total, summed = None, None
    for other, score in enumerate(scores):
        power = jnp.exp2((score - largest) * scale).reshape(own, tile, width)
        term = power * value[other * tile : (other + 1) * tile].astype(jnp.float32)[None]
        total = power if total is None else total + power
        summed = term if summed is None else summed + term
    attended = (summed / total).astype(jnp.bfloat16).reshape(own * tile, width)
    branch = jnp.dot(attended, wo_ref[...], preferred_element_type=jnp.float32)
    branch = branch.reshape(own, tile, width)
    out_ref[0, :, 0] = (mine_ref[:, 0].astype(jnp.float32) + branch).astype(jnp.bfloat16)


def motion(fine, other, chunk, pos, wq, wkv, wo):
    own, rows, cols, width = fine.shape
    others, _, span, _ = other.shape
    tile = min(TILE, span)
    steps = span // tile
    half = rows // 2
    return pl.pallas_call(
        motion_kernel,
        grid=(rows, steps),
        in_specs=[
            pl.BlockSpec((own, 1, tile, width), lambda r, j: (0, r, chunk * steps + j, 0)),
            pl.BlockSpec((others, 1, tile, width), lambda r, j: (0, r, j, 0)),
            pl.BlockSpec(pos.shape, lambda r, j: (0, 0)),
            pl.BlockSpec(wq.shape, lambda r, j: (0, 0)),
            pl.BlockSpec(wkv.shape, lambda r, j: (0, 0)),
            pl.BlockSpec(wo.shape, lambda r, j: (0, 0)),
        ],
        out_specs=pl.BlockSpec((1, own, 1, tile, width), lambda r, j: (r // half, 0, r % half, j, 0)),
        out_shape=jax.ShapeDtypeStruct((2, own, half, span, width), jnp.bfloat16),
        compiler_params=pltpu.CompilerParams(vmem_limit_bytes=48 * 1024 * 1024),
        cost_estimate=pl.CostEstimate(flops=own * rows * span * width * width * 30, bytes_accessed=fine.size * 6 // CHUNKS, transcendentals=own * rows * span * width * 8),
        name="motion",
    )(fine, other, pos, wq, wkv, wo)


def spread_columns(ref, at, row, cols):
    column = lax.broadcasted_iota(jnp.int32, row.shape, 0)
    left = jnp.where(column == 0, 0.0, pltpu.roll(row, 1, 0))
    right = jnp.where(column == cols - 1, 0.0, pltpu.roll(row, cols - 1, 0))
    width = row.shape[1]
    ref[at * cols : (at + 1) * cols, :width] = left.astype(jnp.bfloat16)
    ref[at * cols : (at + 1) * cols, width : 2 * width] = row.astype(jnp.bfloat16)
    ref[at * cols : (at + 1) * cols, 2 * width :] = right.astype(jnp.bfloat16)


def conv_rows(ref, start, count, cols, weight_ref):
    pieces = [ref[(start + step) * cols : (start + step + count) * cols, :] for step in range(3)]
    return jnp.dot(jnp.concatenate(pieces, axis=1), weight_ref[...], preferred_element_type=jnp.float32)


def conv_kernel(chunks, flags_ref, *refs):
    moved_refs = refs[:chunks]
    before_refs = refs[chunks : 2 * chunks]
    after_refs = refs[2 * chunks : 3 * chunks]
    coarse_ref, above_ref, below_ref, lift_ref, w1_ref, w2_ref, out_ref, x_ref, f_ref = refs[3 * chunks :]
    _, rows, cols, width = out_ref.shape
    half = rows // 2
    is_first = flags_ref[0] == 1
    is_last = flags_ref[1] == 1

    def line(r):
        if r < 0:
            parts = [ref[0, r + 2] for ref in before_refs]
        elif r < rows:
            parts = [ref[r // half, 0, r % half] for ref in moved_refs]
        else:
            parts = [ref[0, r - rows] for ref in after_refs]
        return jnp.concatenate(parts, axis=0).astype(jnp.float32)

    for r in range(-2, rows + 2):
        spread_columns(x_ref, r + 2, jnp.maximum(line(r), 0.0), cols)
    for r in range(-1, rows + 1):
        first = conv_rows(x_ref, r + 1, 1, cols, w1_ref)
        first = jnp.maximum(first, 0.0).astype(jnp.bfloat16).astype(jnp.float32)
        if r == -1:
            first = jnp.where(is_first, 0.0, first)
        if r == rows:
            first = jnp.where(is_last, 0.0, first)
        spread_columns(f_ref, r + 1, first, cols)
    top = jnp.where(is_first, coarse_ref[0, 0], above_ref[0, 0])
    bottom = jnp.where(is_last, coarse_ref[0, half - 1], below_ref[0, 0])
    coarse = [top] + [coarse_ref[0, i] for i in range(half)] + [bottom]
    for r in range(rows):
        near = coarse[r // 2 + 1]
        far = coarse[r // 2] if r % 2 == 0 else coarse[r // 2 + 2]
        up = jnp.dot(lift_ref[...], jnp.concatenate([near, far], axis=0), preferred_element_type=jnp.float32)
        second = conv_rows(f_ref, r, 1, cols, w2_ref)
        out_ref[0, r] = (up + line(r) + second).astype(jnp.bfloat16)


def convolutions(flags, moved, before, after, coarse, above, below, lift, w1, w2, rows):
    _, own, half, span, width = moved[0].shape
    chunks = len(moved)
    cols = span * chunks
    small = coarse.shape[2]
    in_specs = [pl.BlockSpec(memory_space=pltpu.SMEM)]
    in_specs += [pl.BlockSpec((2, 1, half, span, width), lambda f: (0, f, 0, 0, 0))] * chunks
    in_specs += [pl.BlockSpec((1, 2, span, width), lambda f: (f, 0, 0, 0))] * (2 * chunks)
    in_specs += [pl.BlockSpec((1, half, small, width), lambda f: (f, 0, 0, 0))]
    in_specs += [pl.BlockSpec((1, 1, small, width), lambda f: (f, 0, 0, 0))] * 2
    in_specs += [pl.BlockSpec(a.shape, lambda f: (0, 0)) for a in (lift, w1, w2)]
    return pl.pallas_call(
        functools.partial(conv_kernel, chunks),
        grid=(own,),
        in_specs=in_specs,
        out_specs=pl.BlockSpec((1, rows, cols, width), lambda f: (f, 0, 0, 0)),
        out_shape=jax.ShapeDtypeStruct((own, rows, cols, width), jnp.bfloat16),
        scratch_shapes=[
            pltpu.VMEM(((rows + 4) * cols, 3 * width), jnp.bfloat16),
            pltpu.VMEM(((rows + 2) * cols, 3 * width), jnp.bfloat16),
        ],
        compiler_params=pltpu.CompilerParams(vmem_limit_bytes=56 * 1024 * 1024),
        cost_estimate=pl.CostEstimate(flops=own * rows * cols * width * width * 45, bytes_accessed=own * rows * cols * width * 8, transcendentals=0),
        name="convolutions",
    )(flags, *moved, *before, *after, coarse, above, below, lift, w1, w2)


def lift_matrix(small):
    out = jnp.arange(2 * small)[:, None]
    source = jnp.arange(small)[None, :]
    near = out // 2
    far = jnp.clip(jnp.where(out % 2 == 0, near - 1, near + 1), 0, small - 1)
    base = 0.75 * (source == near) + 0.25 * (source == far)
    return jnp.concatenate([0.75 * base, 0.25 * base], axis=1).astype(jnp.bfloat16)


def local(fine, coarse, w_query, w_key, w_value, w_out, conv_first, conv_second):
    own, rows, cols, width = fine.shape
    bands, halves = lax.axis_size("space"), lax.axis_size("tm")
    place, mine = lax.axis_index("space"), lax.axis_index("tm")
    up = [(i, i + 1) for i in range(bands - 1)]
    down = [(i + 1, i) for i in range(bands - 1)]
    above = lax.ppermute(coarse[:, -1:], "space", up)
    below = lax.ppermute(coarse[:, :1], "space", down)
    frames = jnp.arange(own, dtype=jnp.int32)
    ids = [lax.rem(mine + shift, halves) * own + frames for shift in range(halves)]
    pos = encode(jnp.concatenate(ids), width)
    wkv = jnp.concatenate([w_key, w_value], axis=1)
    w1 = conv_first.reshape(9 * width, width)
    w2 = conv_second.reshape(9 * width, width)
    flags = jnp.stack([place == 0, place == bands - 1]).astype(jnp.int32)
    span = cols // CHUNKS
    moved, before, after = [], [], []
    for chunk in range(CHUNKS):
        piece = fine[:, :, chunk * span : (chunk + 1) * span]
        rest = []
        for shift in range(1, halves):
            rest.append(lax.ppermute(piece, "tm", [((i + shift) % halves, i) for i in range(halves)]))
        other = rest[0] if len(rest) == 1 else jnp.concatenate(rest, axis=0)
        block = motion(fine, other, chunk, pos, w_query, wkv, w_out)
        moved.append(block)
        before.append(lax.ppermute(block[1][:, -2:], "space", up))
        after.append(lax.ppermute(block[0][:, :2], "space", down))
    return convolutions(flags, moved, before, after, coarse, above, below, lift_matrix(coarse.shape[2]), w1, w2, rows)


def solution(mesh):
    return jax.shard_map(
        local,
        mesh=mesh,
        in_specs=(
            P("tm", "space", None, None),
            P("tm", "space", None, None),
            P(),
            P(),
            P(),
            P(),
            P(),
            P(),
        ),
        out_specs=P("tm", "space", None, None),
        check_vma=False,
    )
```

profile of v0, /device:TPU:21, one launch (start us, length us, event | category | flops | bytes accessed | tf_op | source)
XLA Modules:
  0.0 107.5 jit_solution(17650786650793830981)
XLA Ops:
  0.0 1.9 %fusion.4 = (bf16[4,1,128,256]{3,2,1,0:T(8,128)(2,1)}, bf16[4,1,128,256]{3,2,1,0:T(8,128)(2,1)}) fusion(bf16[4,2,128,256]{3,2,1,0:T(8,128)(2,1)} %refs_12_.1), kind=kLoop, calls=%fused_computation.34 | loop fusion | bytes 1048576 | tf_op jit(solution)/shard_map/slice | solution.py:187
  1.9 3.1 %collective-permute-start.13 = (bf16[4,1,128,256]{3,2,1,0:T(8,128)(2,1)}, bf16[4,1,128,256]{3,2,1,0:T(8,128)(2,1)}, u32[]{:S(2)}, u32[]{:S(2)}) collective-permute-start(bf16[4,1,128,256]{3,2,1,0:T(8,128)(2,1)} %get-tuple-element.9), channel_id=1, source_target_pairs={{1,0},{2,1},{3,2},{4,3},{5,4},{6,5},{7,6},{8,7},{9,8},{10,9},{11,1... | collective-permute-start | bytes 786440 | tf_op jit(solution)/shard_map/ppermute | solution.py:187
  5.0 2.4 %collective-permute-start.12 = (bf16[4,1,128,256]{3,2,1,0:T(8,128)(2,1)}, bf16[4,1,128,256]{3,2,1,0:T(8,128)(2,1)}, u32[]{:S(2)}, u32[]{:S(2)}) collective-permute-start(bf16[4,1,128,256]{3,2,1,0:T(8,128)(2,1)} %get-tuple-element.10), channel_id=1, source_target_pairs={{0,1},{1,2},{2,3},{3,4},{4,5},{5,6},{6,7},{7,8},{8,9},{9,10},{10,1... | collective-permute-start | bytes 786440 | tf_op jit(solution)/shard_map/ppermute | solution.py:186
  7.3 2.9 %fusion.3 = (bf16[4,4,64,256]{3,2,1,0:T(8,128)(2,1)}, bf16[4,4,64,256]{3,2,1,0:T(8,128)(2,1)}, bf16[4,4,64,256]{3,2,1,0:T(8,128)(2,1)}, bf16[4,4,64,256]{3,2,1,0:T(8,128)(2,1)}) fusion(bf16[4,4,256,256]{3,2,1,0:T(8,128)(2,1)} %mine_ref.7), kind=kLoop, calls=%fused_computation.33 | loop fusion | bytes 4194304 | tf_op jit(solution)/shard_map/slice | solution.py:198
  10.2 1.2 %collective-permute-start.3 = (bf16[4,4,64,256]{3,2,1,0:T(8,128)(2,1)}, bf16[4,4,64,256]{3,2,1,0:T(8,128)(2,1)S(1)}, u32[]{:S(2)}, u32[]{:S(2)}) collective-permute-start(bf16[4,4,64,256]{3,2,1,0:T(8,128)(2,1)} %get-tuple-element.5), channel_id=1, source_target_pairs={{16,0},{0,16},{17,1},{1,17},{18,2},{2,18},{19,3},{3,19},{20,4},{4,... | collective-permute-start | bytes 1572872 | tf_op jit(solution)/shard_map/ppermute | solution.py:201
  12.2 0.9 constant_dynamic-update-slice_fusion.wkv_ref
  14.4 1.0 copy-done.8
  15.4 6.0 %motion.7.refs_3_ = bf16[2,4,2,64,256]{4,3,2,1,0:T(8,128)(2,1)S(1)} custom-call(bf16[4,4,256,256]{3,2,1,0:T(8,128)(2,1)S(1)} %copy-done, bf16[4,4,64,256]{3,2,1,0:T(8,128)(2,1)S(1)} %copy-done.8, f32[8,256]{1,0:T(8,128)S(1)} %pad_maximum_fusion.1.pos_ref, bf16[256,256]{1,0:T(8,128)(2,1)S(1)} %copy-done.9, ...), custom_call_target="tpu_custom_call" | custom-call | flops 2013265920 | bytes 1572864 | tf_op jit(solution)/shard_map/motion/pallas_call | solution.py:70
  21.5 0.9 copy-done.5
  22.4 4.0 %collective-permute-start.11 = (bf16[4,2,64,256]{3,2,1,0:T(8,128)(2,1)S(1)}, bf16[4,2,64,256]{3,2,1,0:T(8,128)(2,1)S(1)}, u32[]{:S(2)}, u32[]{:S(2)}) collective-permute-start(bf16[4,2,64,256]{3,2,1,0:T(8,128)(2,1)S(1)} %get-tuple-element.11), channel_id=1, source_target_pairs={{1,0},{2,1},{3,2},{4,3},{5,4},{6,5},{7,6},{8,7},{9,8},{10,9},{11,1... | collective-permute-start | bytes 786440 | tf_op jit(solution)/shard_map/ppermute | solution.py:206
  26.4 1.0 copy-done.6
  27.4 6.0 %motion.6.refs_2_ = bf16[2,4,2,64,256]{4,3,2,1,0:T(8,128)(2,1)S(1)} custom-call(bf16[4,4,256,256]{3,2,1,0:T(8,128)(2,1)S(1)} %copy-done, bf16[4,4,64,256]{3,2,1,0:T(8,128)(2,1)S(1)} %copy-done.6, f32[8,256]{1,0:T(8,128)S(1)} %pad_maximum_fusion.1.pos_ref, bf16[256,256]{1,0:T(8,128)(2,1)S(1)} %copy-done.9, ...), custom_call_target="tpu_custom_call" | custom-call | flops 2013265920 | bytes 1572864 | tf_op jit(solution)/shard_map/motion/pallas_call | solution.py:70
  33.4 2.9 %collective-permute-start.7 = (bf16[4,2,64,256]{3,2,1,0:T(8,128)(2,1)S(1)}, bf16[4,2,64,256]{3,2,1,0:T(8,128)(2,1)S(1)}, u32[]{:S(2)}, u32[]{:S(2)}) collective-permute-start(bf16[4,2,64,256]{3,2,1,0:T(8,128)(2,1)S(1)} %get-tuple-element.12), channel_id=1, source_target_pairs={{0,1},{1,2},{2,3},{3,4},{4,5},{5,6},{6,7},{7,8},{8,9},{9,10},{10,1... | collective-permute-start | bytes 786440 | tf_op jit(solution)/shard_map/ppermute | solution.py:205
  36.3 6.9 %motion.5.refs_1_ = bf16[2,4,2,64,256]{4,3,2,1,0:T(8,128)(2,1)S(1)} custom-call(bf16[4,4,256,256]{3,2,1,0:T(8,128)(2,1)S(1)} %copy-done, bf16[4,4,64,256]{3,2,1,0:T(8,128)(2,1)} %collective-permute-done.1.other_ref, f32[8,256]{1,0:T(8,128)S(1)} %pad_maximum_fusion.1.pos_ref, bf16[256,256]{1,0:T(8,128)(2,1)S(1)} %copy-done.9, ...), custom_call_target="tpu_custom_call" | custom-call | flops 2013265920 | bytes 1572864 | tf_op jit(solution)/shard_map/motion/pallas_call | solution.py:70
  44.1 3.3 %collective-permute-start.10 = (bf16[4,2,64,256]{3,2,1,0:T(8,128)(2,1)S(1)}, bf16[4,2,64,256]{3,2,1,0:T(8,128)(2,1)S(1)}, u32[]{:S(2)}, u32[]{:S(2)}) collective-permute-start(bf16[4,2,64,256]{3,2,1,0:T(8,128)(2,1)S(1)} %get-tuple-element.13), channel_id=1, source_target_pairs={{1,0},{2,1},{3,2},{4,3},{5,4},{6,5},{7,6},{8,7},{9,8},{10,9},{11,1... | collective-permute-start | bytes 786440 | tf_op jit(solution)/shard_map/ppermute | solution.py:206
  47.4 6.0 %motion.4.refs_0_ = bf16[2,4,2,64,256]{4,3,2,1,0:T(8,128)(2,1)S(1)} custom-call(bf16[4,4,256,256]{3,2,1,0:T(8,128)(2,1)S(1)} %copy-done, bf16[4,4,64,256]{3,2,1,0:T(8,128)(2,1)S(1)} %collective-permute-done.other_ref, f32[8,256]{1,0:T(8,128)S(1)} %pad_maximum_fusion.1.pos_ref, bf16[256,256]{1,0:T(8,128)(2,1)S(1)} %copy-done.9, ...), custom_call_target="tpu_custom_call" | custom-call | flops 2013265920 | bytes 1572864 | tf_op jit(solution)/shard_map/motion/pallas_call | solution.py:70
  53.5 3.8 %collective-permute-start.6 = (bf16[4,2,64,256]{3,2,1,0:T(8,128)(2,1)}, bf16[4,2,64,256]{3,2,1,0:T(8,128)(2,1)S(1)}, u32[]{:S(2)}, u32[]{:S(2)}) collective-permute-start(bf16[4,2,64,256]{3,2,1,0:T(8,128)(2,1)} %get-tuple-element.14), channel_id=1, source_target_pairs={{0,1},{1,2},{2,3},{3,4},{4,5},{5,6},{6,7},{7,8},{8,9},{9,10},{10,1... | collective-permute-start | bytes 786440 | tf_op jit(solution)/shard_map/ppermute | solution.py:205
  57.3 2.4 %collective-permute-start.9 = (bf16[4,2,64,256]{3,2,1,0:T(8,128)(2,1)S(1)}, bf16[4,2,64,256]{3,2,1,0:T(8,128)(2,1)S(1)}, u32[]{:S(2)}, u32[]{:S(2)}) collective-permute-start(bf16[4,2,64,256]{3,2,1,0:T(8,128)(2,1)S(1)} %get-tuple-element.15), channel_id=1, source_target_pairs={{1,0},{2,1},{3,2},{4,3},{5,4},{6,5},{7,6},{8,7},{9,8},{10,9},{11,1... | collective-permute-start | bytes 786440 | tf_op jit(solution)/shard_map/ppermute | solution.py:206
  59.8 4.7 %collective-permute-start.5 = (bf16[4,2,64,256]{3,2,1,0:T(8,128)(2,1)S(1)}, bf16[4,2,64,256]{3,2,1,0:T(8,128)(2,1)S(1)}, u32[]{:S(2)}, u32[]{:S(2)}) collective-permute-start(bf16[4,2,64,256]{3,2,1,0:T(8,128)(2,1)S(1)} %get-tuple-element.16), channel_id=1, source_target_pairs={{0,1},{1,2},{2,3},{3,4},{4,5},{5,6},{6,7},{7,8},{8,9},{9,10},{10,1... | collective-permute-start | bytes 786440 | tf_op jit(solution)/shard_map/ppermute | solution.py:205
  64.5 1.9 %collective-permute-start.8 = (bf16[4,2,64,256]{3,2,1,0:T(8,128)(2,1)S(1)}, bf16[4,2,64,256]{3,2,1,0:T(8,128)(2,1)S(1)}, u32[]{:S(2)}, u32[]{:S(2)}) collective-permute-start(bf16[4,2,64,256]{3,2,1,0:T(8,128)(2,1)S(1)} %get-tuple-element.17), channel_id=1, source_target_pairs={{1,0},{2,1},{3,2},{4,3},{5,4},{6,5},{7,6},{8,7},{9,8},{10,9},{11,1... | collective-permute-start | bytes 786440 | tf_op jit(solution)/shard_map/ppermute | solution.py:206
  66.4 5.2 %collective-permute-start.4 = (bf16[4,2,64,256]{3,2,1,0:T(8,128)(2,1)S(1)}, bf16[4,2,64,256]{3,2,1,0:T(8,128)(2,1)S(1)}, u32[]{:S(2)}, u32[]{:S(2)}) collective-permute-start(bf16[4,2,64,256]{3,2,1,0:T(8,128)(2,1)S(1)} %get-tuple-element.18), channel_id=1, source_target_pairs={{0,1},{1,2},{2,3},{3,4},{4,5},{5,6},{6,7},{7,8},{8,9},{9,10},{10,1... | collective-permute-start | bytes 786440 | tf_op jit(solution)/shard_map/ppermute | solution.py:205
  73.1 11.2 %collective-permute-done.9.refs_9_ = bf16[4,2,64,256]{3,2,1,0:T(8,128)(2,1)S(1)} collective-permute-done((bf16[4,2,64,256]{3,2,1,0:T(8,128)(2,1)S(1)}, bf16[4,2,64,256]{3,2,1,0:T(8,128)(2,1)S(1)}, u32[]{:S(2)}, u32[]{:S(2)}) %collective-permute-start.9) | collective-permute-done | bytes 262176 | tf_op jit(solution)/shard_map/ppermute | solution.py:206
  84.3 5.6 %collective-permute-done.8.refs_8_ = bf16[4,2,64,256]{3,2,1,0:T(8,128)(2,1)S(1)} collective-permute-done((bf16[4,2,64,256]{3,2,1,0:T(8,128)(2,1)S(1)}, bf16[4,2,64,256]{3,2,1,0:T(8,128)(2,1)S(1)}, u32[]{:S(2)}, u32[]{:S(2)}) %collective-permute-start.8) | collective-permute-done | bytes 262176 | tf_op jit(solution)/shard_map/ppermute | solution.py:206
  90.7 16.8 %convolutions.1 = bf16[4,4,256,256]{3,2,1,0:T(8,128)(2,1)} custom-call(s32[2]{0:T(128)} %add_convert_fusion.flags_ref, bf16[2,4,2,64,256]{4,3,2,1,0:T(8,128)(2,1)} %copy-done.4, bf16[2,4,2,64,256]{4,3,2,1,0:T(8,128)(2,1)} %copy-done.3, bf16[2,4,2,64,256]{4,3,2,1,0:T(8,128)(2,1)} %copy-done.2, bf16[2,4,2,64,256]{4,3,2,1,0:T(8,128)(2,1)} %copy-done.1, ...), custom_call_target="tpu_custom_call" | custom-call | flops 12079595520 | bytes 8388608 | tf_op jit(solution)/shard_map/convolutions/pallas_call | solution.py:155
  (66 shorter events, 5.2 us)
Async XLA Ops:
  1.9 51.7 %collective-permute-start.13 = (bf16[4,1,128,256]{3,2,1,0:T(8,128)(2,1)}, bf16[4,1,128,256]{3,2,1,0:T(8,128)(2,1)}, u32[]{:S(2)}, u32[]{:S(2)}) collective-permute-start(bf16[4,1,128,256]{3,2,1,0:T(8,128)(2,1)} %get-tuple-element.9), channel_id=1, source_target_pairs={{1,0},{2,1},{3,2},{4,3},{5,4},{6,5},{7,6},{8,7},{9,8},{10,9},{11,1... | collective-permute-start | bytes 786440 | tf_op jit(solution)/shard_map/ppermute | solution.py:187
  4.9 7.3 %copy-start.11 = (bf16[256,256]{1,0:T(8,128)(2,1)S(1)}, bf16[256,256]{1,0:T(8,128)(2,1)}, u32[]{:S(2)}) copy-start(bf16[256,256]{1,0:T(8,128)(2,1)} %param.11) | copy-start | bytes 393220
  4.9 9.4 %copy-start = (bf16[4,4,256,256]{3,2,1,0:T(8,128)(2,1)S(1)}, bf16[4,4,256,256]{3,2,1,0:T(8,128)(2,1)}, u32[]{:S(2)}) copy-start(bf16[4,4,256,256]{3,2,1,0:T(8,128)(2,1)} %mine_ref.7) | copy-start | bytes 6291460
  4.9 9.4 %copy-start.9 = (bf16[256,256]{1,0:T(8,128)(2,1)S(1)}, bf16[256,256]{1,0:T(8,128)(2,1)}, u32[]{:S(2)}) copy-start(bf16[256,256]{1,0:T(8,128)(2,1)} %wq_ref.7) | copy-start | bytes 393220
  5.0 9.4 %copy-start.10 = (bf16[256,256]{1,0:T(8,128)(2,1)S(1)}, bf16[256,256]{1,0:T(8,128)(2,1)}, u32[]{:S(2)}) copy-start(bf16[256,256]{1,0:T(8,128)(2,1)} %wo_ref.7) | copy-start | bytes 393220
  5.0 52.4 %collective-permute-start.12 = (bf16[4,1,128,256]{3,2,1,0:T(8,128)(2,1)}, bf16[4,1,128,256]{3,2,1,0:T(8,128)(2,1)}, u32[]{:S(2)}, u32[]{:S(2)}) collective-permute-start(bf16[4,1,128,256]{3,2,1,0:T(8,128)(2,1)} %get-tuple-element.10), channel_id=1, source_target_pairs={{0,1},{1,2},{2,3},{3,4},{4,5},{5,6},{6,7},{7,8},{8,9},{9,10},{10,1... | collective-permute-start | bytes 786440 | tf_op jit(solution)/shard_map/ppermute | solution.py:186
  10.2 3.0 %collective-permute-start.3 = (bf16[4,4,64,256]{3,2,1,0:T(8,128)(2,1)}, bf16[4,4,64,256]{3,2,1,0:T(8,128)(2,1)S(1)}, u32[]{:S(2)}, u32[]{:S(2)}) collective-permute-start(bf16[4,4,64,256]{3,2,1,0:T(8,128)(2,1)} %get-tuple-element.5), channel_id=1, source_target_pairs={{16,0},{0,16},{17,1},{1,17},{18,2},{2,18},{19,3},{3,19},{20,4},{4,... | collective-permute-start | bytes 1572872 | tf_op jit(solution)/shard_map/ppermute | solution.py:201
  11.5 10.0 %collective-permute-start.2 = (bf16[4,4,64,256]{3,2,1,0:T(8,128)(2,1)}, bf16[4,4,64,256]{3,2,1,0:T(8,128)(2,1)S(1)}, u32[]{:S(2)}, u32[]{:S(2)}) collective-permute-start(bf16[4,4,64,256]{3,2,1,0:T(8,128)(2,1)} %get-tuple-element.6), channel_id=1, source_target_pairs={{16,0},{0,16},{17,1},{1,17},{18,2},{2,18},{19,3},{3,19},{20,4},{4,... | collective-permute-start | bytes 1572872 | tf_op jit(solution)/shard_map/ppermute | solution.py:201
  11.5 22.0 %collective-permute-start.1 = (bf16[4,4,64,256]{3,2,1,0:T(8,128)(2,1)}, bf16[4,4,64,256]{3,2,1,0:T(8,128)(2,1)}, u32[]{:S(2)}, u32[]{:S(2)}) collective-permute-start(bf16[4,4,64,256]{3,2,1,0:T(8,128)(2,1)} %get-tuple-element.7), channel_id=1, source_target_pairs={{16,0},{0,16},{17,1},{1,17},{18,2},{2,18},{19,3},{3,19},{20,4},{4,... | collective-permute-start | bytes 1572872 | tf_op jit(solution)/shard_map/ppermute | solution.py:201
  14.0 30.1 %collective-permute-start = (bf16[4,4,64,256]{3,2,1,0:T(8,128)(2,1)}, bf16[4,4,64,256]{3,2,1,0:T(8,128)(2,1)S(1)}, u32[]{:S(2)}, u32[]{:S(2)}) collective-permute-start(bf16[4,4,64,256]{3,2,1,0:T(8,128)(2,1)} %get-tuple-element.8), channel_id=1, source_target_pairs={{16,0},{0,16},{17,1},{1,17},{18,2},{2,18},{19,3},{3,19},{20,4},{4,... | collective-permute-start | bytes 1572872 | tf_op jit(solution)/shard_map/ppermute | solution.py:201
  21.4 12.0 %copy-start.1 = (bf16[2,4,2,64,256]{4,3,2,1,0:T(8,128)(2,1)}, bf16[2,4,2,64,256]{4,3,2,1,0:T(8,128)(2,1)S(1)}, u32[]{:S(2)}) copy-start(bf16[2,4,2,64,256]{4,3,2,1,0:T(8,128)(2,1)S(1)} %motion.7.refs_3_) | copy-start | bytes 1572868
  22.4 37.4 %collective-permute-start.11 = (bf16[4,2,64,256]{3,2,1,0:T(8,128)(2,1)S(1)}, bf16[4,2,64,256]{3,2,1,0:T(8,128)(2,1)S(1)}, u32[]{:S(2)}, u32[]{:S(2)}) collective-permute-start(bf16[4,2,64,256]{3,2,1,0:T(8,128)(2,1)S(1)} %get-tuple-element.11), channel_id=1, source_target_pairs={{1,0},{2,1},{3,2},{4,3},{5,4},{6,5},{7,6},{8,7},{9,8},{10,9},{11,1... | collective-permute-start | bytes 786440 | tf_op jit(solution)/shard_map/ppermute | solution.py:206
  33.4 9.8 %copy-start.2 = (bf16[2,4,2,64,256]{4,3,2,1,0:T(8,128)(2,1)}, bf16[2,4,2,64,256]{4,3,2,1,0:T(8,128)(2,1)S(1)}, u32[]{:S(2)}) copy-start(bf16[2,4,2,64,256]{4,3,2,1,0:T(8,128)(2,1)S(1)} %motion.6.refs_2_) | copy-start | bytes 1572868
  33.4 31.0 %collective-permute-start.7 = (bf16[4,2,64,256]{3,2,1,0:T(8,128)(2,1)S(1)}, bf16[4,2,64,256]{3,2,1,0:T(8,128)(2,1)S(1)}, u32[]{:S(2)}, u32[]{:S(2)}) collective-permute-start(bf16[4,2,64,256]{3,2,1,0:T(8,128)(2,1)S(1)} %get-tuple-element.12), channel_id=1, source_target_pairs={{0,1},{1,2},{2,3},{3,4},{4,5},{5,6},{6,7},{7,8},{8,9},{9,10},{10,1... | collective-permute-start | bytes 786440 | tf_op jit(solution)/shard_map/ppermute | solution.py:205
  43.2 10.2 %copy-start.3 = (bf16[2,4,2,64,256]{4,3,2,1,0:T(8,128)(2,1)}, bf16[2,4,2,64,256]{4,3,2,1,0:T(8,128)(2,1)S(1)}, u32[]{:S(2)}) copy-start(bf16[2,4,2,64,256]{4,3,2,1,0:T(8,128)(2,1)S(1)} %motion.5.refs_1_) | copy-start | bytes 1572868
  44.1 22.3 %collective-permute-start.10 = (bf16[4,2,64,256]{3,2,1,0:T(8,128)(2,1)S(1)}, bf16[4,2,64,256]{3,2,1,0:T(8,128)(2,1)S(1)}, u32[]{:S(2)}, u32[]{:S(2)}) collective-permute-start(bf16[4,2,64,256]{3,2,1,0:T(8,128)(2,1)S(1)} %get-tuple-element.13), channel_id=1, source_target_pairs={{1,0},{2,1},{3,2},{4,3},{5,4},{6,5},{7,6},{8,7},{9,8},{10,9},{11,1... | collective-permute-start | bytes 786440 | tf_op jit(solution)/shard_map/ppermute | solution.py:206
  53.5 36.4 %copy-start.4 = (bf16[2,4,2,64,256]{4,3,2,1,0:T(8,128)(2,1)}, bf16[2,4,2,64,256]{4,3,2,1,0:T(8,128)(2,1)S(1)}, u32[]{:S(2)}) copy-start(bf16[2,4,2,64,256]{4,3,2,1,0:T(8,128)(2,1)S(1)} %motion.4.refs_0_) | copy-start | bytes 1572868
  53.5 19.6 %collective-permute-start.6 = (bf16[4,2,64,256]{3,2,1,0:T(8,128)(2,1)}, bf16[4,2,64,256]{3,2,1,0:T(8,128)(2,1)S(1)}, u32[]{:S(2)}, u32[]{:S(2)}) collective-permute-start(bf16[4,2,64,256]{3,2,1,0:T(8,128)(2,1)} %get-tuple-element.14), channel_id=1, source_target_pairs={{0,1},{1,2},{2,3},{3,4},{4,5},{5,6},{6,7},{7,8},{8,9},{9,10},{10,1... | collective-permute-start | bytes 786440 | tf_op jit(solution)/shard_map/ppermute | solution.py:205
  57.3 26.9 %collective-permute-start.9 = (bf16[4,2,64,256]{3,2,1,0:T(8,128)(2,1)S(1)}, bf16[4,2,64,256]{3,2,1,0:T(8,128)(2,1)S(1)}, u32[]{:S(2)}, u32[]{:S(2)}) collective-permute-start(bf16[4,2,64,256]{3,2,1,0:T(8,128)(2,1)S(1)} %get-tuple-element.15), channel_id=1, source_target_pairs={{1,0},{2,1},{3,2},{4,3},{5,4},{6,5},{7,6},{8,7},{9,8},{10,9},{11,1... | collective-permute-start | bytes 786440 | tf_op jit(solution)/shard_map/ppermute | solution.py:206
  59.8 11.8 %copy-start.12 = (bf16[4,2,64,256]{3,2,1,0:T(8,128)(2,1)}, bf16[4,2,64,256]{3,2,1,0:T(8,128)(2,1)S(1)}, u32[]{:S(2)}) copy-start(bf16[4,2,64,256]{3,2,1,0:T(8,128)(2,1)S(1)} %collective-permute-done.11.refs_11_) | copy-start | bytes 786436
  59.8 24.5 %collective-permute-start.5 = (bf16[4,2,64,256]{3,2,1,0:T(8,128)(2,1)S(1)}, bf16[4,2,64,256]{3,2,1,0:T(8,128)(2,1)S(1)}, u32[]{:S(2)}, u32[]{:S(2)}) collective-permute-start(bf16[4,2,64,256]{3,2,1,0:T(8,128)(2,1)S(1)} %get-tuple-element.16), channel_id=1, source_target_pairs={{0,1},{1,2},{2,3},{3,4},{4,5},{5,6},{6,7},{7,8},{8,9},{9,10},{10,1... | collective-permute-start | bytes 786440 | tf_op jit(solution)/shard_map/ppermute | solution.py:205
  64.5 25.4 %collective-permute-start.8 = (bf16[4,2,64,256]{3,2,1,0:T(8,128)(2,1)S(1)}, bf16[4,2,64,256]{3,2,1,0:T(8,128)(2,1)S(1)}, u32[]{:S(2)}, u32[]{:S(2)}) collective-permute-start(bf16[4,2,64,256]{3,2,1,0:T(8,128)(2,1)S(1)} %get-tuple-element.17), channel_id=1, source_target_pairs={{1,0},{2,1},{3,2},{4,3},{5,4},{6,5},{7,6},{8,7},{9,8},{10,9},{11,1... | collective-permute-start | bytes 786440 | tf_op jit(solution)/shard_map/ppermute | solution.py:206
  66.4 23.5 %collective-permute-start.4 = (bf16[4,2,64,256]{3,2,1,0:T(8,128)(2,1)S(1)}, bf16[4,2,64,256]{3,2,1,0:T(8,128)(2,1)S(1)}, u32[]{:S(2)}, u32[]{:S(2)}) collective-permute-start(bf16[4,2,64,256]{3,2,1,0:T(8,128)(2,1)S(1)} %get-tuple-element.18), channel_id=1, source_target_pairs={{0,1},{1,2},{2,3},{3,4},{4,5},{5,6},{6,7},{7,8},{8,9},{9,10},{10,1... | collective-permute-start | bytes 786440 | tf_op jit(solution)/shard_map/ppermute | solution.py:205
  73.1 16.8 %copy-start.15 = (bf16[4,2,64,256]{3,2,1,0:T(8,128)(2,1)}, bf16[4,2,64,256]{3,2,1,0:T(8,128)(2,1)S(1)}, u32[]{:S(2)}) copy-start(bf16[4,2,64,256]{3,2,1,0:T(8,128)(2,1)S(1)} %collective-permute-done.6.refs_6_) | copy-start | bytes 786436
  (10 other events, 28.9 us)
where the time goes:
time: 108 us; the launch traced here: 107 us
  Pallas kernels  41.7 us (39%)
  starting transfers between devices  35.6 us (33%)
  waiting for transfers between devices  16.9 us (16%)
  local copies, waits for them, and re-layouts  11.2 us (10%)
  other arithmetic  1.68 us (2%)
    pallas_call x4, Pallas kernels, motion(): pl.pallas_call(motion_kernel, grid=(rows, steps), in_specs=[pl.BlockSpec(...  25 us
    ppermute x4, waiting for transfers between devices, local(): after.append(lax.ppermute(block[0][:, :2], 'space', down))  16.8 us
    pallas_call x1, Pallas kernels, convolutions(): pl.pallas_call(functools.partial(conv_kernel, chunks), grid=(own,), in_sp...  16.8 us
    ppermute x4, starting transfers between devices, local(): before.append(lax.ppermute(block[1][:, -2:], 'space', up))  16.5 us
    ppermute x4, starting transfers between devices, local(): after.append(lax.ppermute(block[0][:, :2], 'space', down))  11.6 us
    unnamed x41, local copies, waits for them, and re-layouts  4.58 us
    ppermute x1, starting transfers between devices, local(): below = lax.ppermute(coarse[:, :1], 'space', down)  3.05 us
    slice x1, local copies, waits for them, and re-layouts, local(): piece = fine[:, :, chunk * span:(chunk + 1) * span]  2.89 us
  transfers between devices with their start and end apart: 14, of which 3 were waited for; matrix products, arithmetic and copies ran while one was open for 6% of the time, Pallas kernels for 23%

commit v1 on v0

v1 whole, which is shorter than its diff:
```python
import functools

import jax
import jax.numpy as jnp
import numpy as np
from jax import lax
from jax.experimental import pallas as pl
from jax.experimental.pallas import tpu as pltpu
from jax.sharding import PartitionSpec as P

HEADS = 8
CHUNKS = 4
HALO = 2
LOG2E = 1.4426950408889634
MESH = pl.DeviceIdType.MESH


def encode(frames, width):
    half = width // 2
    inverse = np.exp(-np.log(10000.0) * 2.0 * np.arange(half) / width)
    angles = np.arange(frames)[:, None] * inverse[None, :]
    return np.concatenate([np.sin(angles), np.cos(angles)], axis=1).astype(np.float32)


def lift_matrix(small):
    out = np.arange(2 * small)[:, None]
    source = np.arange(small)[None, :]
    near = out // 2
    far = np.clip(np.where(out % 2 == 0, near - 1, near + 1), 0, small - 1)
    base = 0.75 * (source == near) + 0.25 * (source == far)
    return np.concatenate([0.75 * base, 0.25 * base], axis=1).astype(jnp.bfloat16)


def attention(mine, others, pos, wq_ref, wk_ref, wv_ref, wo_ref):
    own, (tile, width) = len(mine), mine[0].shape
    depth = width // HEADS
    scale = LOG2E / (float(depth) ** 0.5)
    normed = []
    for x, place in zip(mine + others, pos):
        hidden = x.astype(jnp.float32) + place
        center = hidden - jnp.mean(hidden, axis=-1, keepdims=True)
        spread = jnp.mean(center * center, axis=-1, keepdims=True)
        normed.append((center * lax.rsqrt(spread + 1e-05)).astype(jnp.bfloat16))
    flat = jnp.concatenate(normed, axis=0)
    query = jnp.dot(flat[: own * tile], wq_ref[...], preferred_element_type=jnp.float32)
    query = query.astype(jnp.bfloat16).reshape(own, tile, width)
    key = jnp.dot(flat, wk_ref[...], preferred_element_type=jnp.float32).astype(jnp.bfloat16)
    value = jnp.dot(flat, wv_ref[...], preferred_element_type=jnp.float32).astype(jnp.bfloat16)
    rows = lax.broadcasted_iota(jnp.int32, (width, width), 0) // depth
    cols = lax.broadcasted_iota(jnp.int32, (width, width), 1) // depth
    blocks = jnp.where(rows == cols, 1.0, 0.0).astype(jnp.bfloat16)
    scores = []
    for at in range(len(normed)):
        product = query * key[at * tile : (at + 1) * tile][None]
        scores.append(jnp.dot(product.reshape(own * tile, width), blocks, preferred_element_type=jnp.float32))
    largest = functools.reduce(jnp.maximum, scores)
    total, summed = None, None
    for at, score in enumerate(scores):
        power = jnp.exp2((score - largest) * scale).reshape(own, tile, width)
        term = power * value[at * tile : (at + 1) * tile].astype(jnp.float32)[None]
        total = power if total is None else total + power
        summed = term if summed is None else summed + term
    attended = (summed / total).astype(jnp.bfloat16).reshape(own * tile, width)
    branch = jnp.dot(attended, wo_ref[...], preferred_element_type=jnp.float32)
    return branch.reshape(own, tile, width)


def spread_columns(ref, at, row, cols):
    column = lax.broadcasted_iota(jnp.int32, row.shape, 0)
    left = jnp.where(column == 0, 0.0, pltpu.roll(row, 1, 0))
    right = jnp.where(column == cols - 1, 0.0, pltpu.roll(row, cols - 1, 0))
    width = row.shape[1]
    ref[at * cols : (at + 1) * cols, :width] = left.astype(jnp.bfloat16)
    ref[at * cols : (at + 1) * cols, width : 2 * width] = row.astype(jnp.bfloat16)
    ref[at * cols : (at + 1) * cols, 2 * width :] = right.astype(jnp.bfloat16)


def conv_rows(ref, start, count, cols, weight_ref):
    pieces = [ref[(start + step) * cols : (start + step + count) * cols, :] for step in range(3)]
    return jnp.dot(jnp.concatenate(pieces, axis=1), weight_ref[...], preferred_element_type=jnp.float32)


def kernel(
    bands, halves, fine_ref, coarse_ref, pos_ref, wq_ref, wk_ref, wv_ref, wo_ref, w1_hbm, w2_hbm, lift_ref, out_ref,
    mine, other, moved, coarse, x_ref, f_ref, w1_ref, w2_ref, outs,
    local_sems, fine_send, fine_recv, halo_send, halo_recv, coarse_send, coarse_recv, out_sems,
):
    own, rows, cols, width = mine.shape
    half = rows // 2
    span = cols // CHUNKS
    early = own // 2
    place, core = lax.axis_index("space"), lax.axis_index("tm")
    has_before, has_after = place > 0, place < bands - 1

    def fine_copy(shift, chunk):
        span_at = pl.ds(pl.multiple_of(chunk * span, span), span)
        return pltpu.make_async_remote_copy(
            src_ref=fine_ref.at[:, :, span_at],
            dst_ref=other.at[pl.ds((shift - 1) * own, own), :, span_at],
            send_sem=fine_send.at[shift - 1, chunk],
            recv_sem=fine_recv.at[shift - 1, chunk],
            device_id={"tm": lax.rem(core + halves - shift, halves)},
            device_id_type=MESH,
        )

    def mine_copy(chunk):
        span_at = pl.ds(pl.multiple_of(chunk * span, span), span)
        return pltpu.make_async_copy(fine_ref.at[:, :, span_at], mine.at[:, :, span_at], local_sems.at[chunk])

    def to_after(src, dst, send, recv):
        return pltpu.make_async_remote_copy(
            src_ref=src, dst_ref=dst, send_sem=send, recv_sem=recv, device_id={"space": place + 1}, device_id_type=MESH
        )

    def to_before(src, dst, send, recv):
        return pltpu.make_async_remote_copy(
            src_ref=src, dst_ref=dst, send_sem=send, recv_sem=recv, device_id={"space": place - 1}, device_id_type=MESH
        )

    def coarse_up():
        return to_after(coarse_ref.at[:, half - 1 : half], coarse.at[:, 0:1], coarse_send.at[0], coarse_recv.at[0])

    def coarse_down():
        return to_before(coarse_ref.at[:, 0:1], coarse.at[:, half + 1 : half + 2], coarse_send.at[1], coarse_recv.at[1])

    def halo_up(frames, span_at, piece):
        return to_after(
            moved.at[frames, rows : rows + HALO, span_at], moved.at[frames, 0:HALO, span_at],
            halo_send.at[0, piece], halo_recv.at[0, piece],
        )

    def halo_down(frames, span_at, piece):
        return to_before(
            moved.at[frames, HALO : 2 * HALO, span_at], moved.at[frames, rows + HALO : rows + 2 * HALO, span_at],
            halo_send.at[1, piece], halo_recv.at[1, piece],
        )

    def both(frames, span_at, piece, act_up, act_down):
        pl.when(has_after)(lambda: act_up(halo_up(frames, span_at, piece)))
        pl.when(has_before)(lambda: act_down(halo_down(frames, span_at, piece)))

    def start(copy):
        copy.start()

    def wait_send(copy):
        copy.wait_send()

    def wait_recv(copy):
        copy.wait_recv()

    def landed(frames, span_at, piece):
        pl.when(has_before)(lambda: halo_up(frames, span_at, piece).wait_recv())
        pl.when(has_after)(lambda: halo_down(frames, span_at, piece).wait_recv())

    for chunk in range(CHUNKS):
        mine_copy(chunk).start()
    own_coarse = pltpu.make_async_copy(coarse_ref, coarse.at[:, 1 : half + 1], local_sems.at[CHUNKS])
    first_weights = pltpu.make_async_copy(w1_hbm, w1_ref, local_sems.at[CHUNKS + 1])
    second_weights = pltpu.make_async_copy(w2_hbm, w2_ref, local_sems.at[CHUNKS + 2])

    barrier = pltpu.get_barrier_semaphore()
    for shift in range(1, halves):
        pl.semaphore_signal(barrier, inc=1, device_id={"tm": lax.rem(core + shift, halves)}, device_id_type=MESH)

    @pl.when(has_before)
    def _():
        pl.semaphore_signal(barrier, inc=1, device_id={"space": place - 1}, device_id_type=MESH)

    @pl.when(has_after)
    def _():
        pl.semaphore_signal(barrier, inc=1, device_id={"space": place + 1}, device_id_type=MESH)

    peers = halves - 1 + has_before.astype(jnp.int32) + has_after.astype(jnp.int32)
    pl.semaphore_wait(barrier, peers)

    for shift in range(1, halves):
        for chunk in range(CHUNKS):
            fine_copy(shift, chunk).start()
    pl.when(has_after)(lambda: coarse_up().start())
    pl.when(has_before)(lambda: coarse_down().start())
    own_coarse.start()
    first_weights.start()
    second_weights.start()

    @pl.when(jnp.logical_not(has_before))
    def _():
        moved[:, 0:HALO] = jnp.zeros((own, HALO, cols, width), jnp.bfloat16)

    @pl.when(jnp.logical_not(has_after))
    def _():
        moved[:, rows + HALO :] = jnp.zeros((own, HALO, cols, width), jnp.bfloat16)

    pos = []
    for shift in range(halves):
        for frame in range(own):
            pos.append(pos_ref[pl.ds(lax.rem(core + shift, halves) * own + frame, 1), :])

    def motion_step(step, carry):
        chunk, row = step // rows, lax.rem(step, rows)
        span_at = pl.ds(pl.multiple_of(chunk * span, span), span)

        @pl.when(row == 0)
        def _():
            mine_copy(chunk).wait()
            for shift in range(1, halves):
                fine_copy(shift, chunk).wait_recv()

        here = [mine[frame, row, span_at, :] for frame in range(own)]
        there = [other[frame, row, span_at, :] for frame in range(own * (halves - 1))]
        branch = attention(here, there, pos, wq_ref, wk_ref, wv_ref, wo_ref)
        for frame in range(own):
            moved[frame, row + HALO, span_at, :] = (here[frame].astype(jnp.float32) + branch[frame]).astype(jnp.bfloat16)

        @pl.when((row == rows - 1) & (chunk == 0))
        def _():
            both(pl.ds(0, own), pl.ds(0, span), 0, start, start)

        @pl.when((row == rows - 1) & (chunk > 0))
        def _():
            both(pl.ds(0, early), span_at, chunk, start, start)

        return carry

    lax.fori_loop(0, CHUNKS * rows, motion_step, 0)
    rest = pl.ds(span, cols - span)
    for frame in range(early, own):
        both(pl.ds(frame, 1), rest, CHUNKS + frame - early, start, start)

    own_coarse.wait()
    first_weights.wait()
    second_weights.wait()
    pl.when(has_before)(lambda: coarse_up().wait_recv())
    pl.when(has_after)(lambda: coarse_down().wait_recv())

    @pl.when(jnp.logical_not(has_before))
    def _():
        coarse[:, 0] = coarse[:, 1]

    @pl.when(jnp.logical_not(has_after))
    def _():
        coarse[:, half + 1] = coarse[:, half]

    def out_copy(frame):
        slot = lax.rem(frame, 2)
        return pltpu.make_async_copy(outs.at[slot], out_ref.at[frame], out_sems.at[slot])

    def conv_step(frame, carry):
        @pl.when(frame == 0)
        def _():
            landed(pl.ds(0, own), pl.ds(0, span), 0)
            for chunk in range(1, CHUNKS):
                landed(pl.ds(0, early), pl.ds(chunk * span, span), chunk)

        @pl.when(frame >= early)
        def _():
            landed(pl.ds(frame, 1), rest, CHUNKS + frame - early)

        for r in range(rows + 2 * HALO):
            spread_columns(x_ref, r, jnp.maximum(moved[frame, r].astype(jnp.float32), 0.0), cols)
        for r in range(rows + 2):
            first = conv_rows(x_ref, r, 1, cols, w1_ref)
            first = jnp.maximum(first, 0.0).astype(jnp.bfloat16).astype(jnp.float32)
            if r == 0:
                first = jnp.where(has_before, first, 0.0)
            if r == rows + 1:
                first = jnp.where(has_after, first, 0.0)
            spread_columns(f_ref, r, first, cols)

        @pl.when(frame >= 2)
        def _():
            out_copy(frame - 2).wait()

        for r in range(rows):
            near = coarse[frame, r // 2 + 1]
            far = coarse[frame, r // 2] if r % 2 == 0 else coarse[frame, r // 2 + 2]
            up = jnp.dot(lift_ref[...], jnp.concatenate([near, far], axis=0), preferred_element_type=jnp.float32)
            second = conv_rows(f_ref, r, 1, cols, w2_ref)
            outs[lax.rem(frame, 2), r] = (up + moved[frame, r + HALO].astype(jnp.float32) + second).astype(jnp.bfloat16)
        out_copy(frame).start()
        return carry

    lax.fori_loop(0, own, conv_step, 0)
    for frame in range(max(own - 2, 0), own):
        out_copy(frame).wait()
    for shift in range(1, halves):
        for chunk in range(CHUNKS):
            fine_copy(shift, chunk).wait_send()
    pl.when(has_after)(lambda: coarse_up().wait_send())
    pl.when(has_before)(lambda: coarse_down().wait_send())
    both(pl.ds(0, own), pl.ds(0, span), 0, wait_send, wait_send)
    for chunk in range(1, CHUNKS):
        both(pl.ds(0, early), pl.ds(chunk * span, span), chunk, wait_send, wait_send)
    for frame in range(early, own):
        both(pl.ds(frame, 1), rest, CHUNKS + frame - early, wait_send, wait_send)


def local(fine, coarse, w_query, w_key, w_value, w_out, conv_first, conv_second):
    own, rows, cols, width = fine.shape
    _, half, small, _ = coarse.shape
    bands, halves = lax.axis_size("space"), lax.axis_size("tm")
    pieces = CHUNKS + own - own // 2
    far = own * (halves - 1)
    any_space = pl.BlockSpec(memory_space=pl.ANY)
    vmem = pl.BlockSpec(memory_space=pltpu.VMEM)
    bf16 = jnp.bfloat16
    return pl.pallas_call(
        functools.partial(kernel, bands, halves),
        in_specs=[any_space] * 2 + [vmem] * 5 + [any_space] * 2 + [vmem],
        out_specs=any_space,
        out_shape=jax.ShapeDtypeStruct(fine.shape, bf16),
        scratch_shapes=[
            pltpu.VMEM((own, rows, cols, width), bf16),
            pltpu.VMEM((far, rows, cols, width), bf16),
            pltpu.VMEM((own, rows + 2 * HALO, cols, width), bf16),
            pltpu.VMEM((own, half + 2, small, width), bf16),
            pltpu.VMEM(((rows + 4) * cols, 3 * width), bf16),
            pltpu.VMEM(((rows + 2) * cols, 3 * width), bf16),
            pltpu.VMEM((9 * width, width), bf16),
            pltpu.VMEM((9 * width, width), bf16),
            pltpu.VMEM((2, rows, cols, width), bf16),
            pltpu.SemaphoreType.DMA((CHUNKS + 3,)),
            pltpu.SemaphoreType.DMA((halves - 1, CHUNKS)),
            pltpu.SemaphoreType.DMA((halves - 1, CHUNKS)),
            pltpu.SemaphoreType.DMA((2, pieces)),
            pltpu.SemaphoreType.DMA((2, pieces)),
            pltpu.SemaphoreType.DMA((2,)),
            pltpu.SemaphoreType.DMA((2,)),
            pltpu.SemaphoreType.DMA((2,)),
        ],
        compiler_params=pltpu.CompilerParams(
            collective_id=0, has_side_effects=True, vmem_limit_bytes=62 * 1024 * 1024
        ),
        name="fused",
    )(
        fine, coarse, jnp.asarray(encode(own * halves, width)), w_query, w_key, w_value, w_out,
        conv_first.reshape(9 * width, width), conv_second.reshape(9 * width, width), jnp.asarray(lift_matrix(small)),
    )


def solution(mesh):
    return jax.shard_map(
        local,
        mesh=mesh,
        in_specs=(
            P("tm", "space", None, None),
            P("tm", "space", None, None),
            P(),
            P(),
            P(),
            P(),
            P(),
            P(),
        ),
        out_specs=P("tm", "space", None, None),
        check_vma=False,
    )
```

time: 108 us -> 72.5 us (0.67)
  starting transfers between devices: 35.6 us -> 0 us
  Pallas kernels: 41.7 us -> 68.3 us
  waiting for transfers between devices: 16.9 us -> 0 us
  local copies, waits for them, and re-layouts: 11.2 us -> 3.1 us
  other arithmetic: 1.68 us -> 0 us
    ppermute x14 -> x0, starting transfers between devices: 35.6 us -> none  [the longest x4 16.5 us: local(): before.append(lax.ppermute(block[1][:, -2:], 'space', up))]
    pallas_call x5 -> x1, Pallas kernels: 41.7 us -> 68.3 us  [local(): pl.pallas_call(functools.partial(kernel, bands, halves), in_specs=[any_sp...]
    ppermute x14 -> x0, waiting for transfers between devices: 16.9 us -> none  [the longest x4 16.8 us: local(): after.append(lax.ppermute(block[0][:, :2], 'space', down))]
    slice x2 -> x0, local copies, waits for them, and re-layouts: 4.75 us -> none  [the longest x1 2.89 us: local(): piece = fine[:, :, chunk * span:(chunk + 1) * span]]
    unnamed x41 -> x1, local copies, waits for them, and re-layouts: 4.58 us -> 3.1 us
  transfers between devices with their start and end apart: 14 -> 0, of which waited for: 3 -> 0; matrix products, arithmetic and copies ran while one was open for 6% -> 0% of each run, Pallas kernels for 23% -> 0%
where the time goes in v1:
time: 72.5 us; the launch traced here: 71.4 us
  Pallas kernels  68.3 us (94%)
  local copies, waits for them, and re-layouts  3.1 us (4%)
    pallas_call x1, Pallas kernels, local(): pl.pallas_call(functools.partial(kernel, bands, halves), in_specs=[any_sp...  68.3 us
    unnamed x1, local copies, waits for them, and re-layouts  3.1 us

profile of v1, /device:TPU:21, one launch (start us, length us, event | category | flops | bytes accessed | tf_op | source)
XLA Modules:
  0.0 71.4 jit_solution(14426534260480697510)
XLA Ops:
  0.0 68.3 %fused.1 = bf16[4,4,256,256]{3,2,1,0:T(8,128)(2,1)} custom-call(bf16[4,4,256,256]{3,2,1,0:T(8,128)(2,1)} %fine_ref.1, bf16[4,2,128,256]{3,2,1,0:T(8,128)(2,1)} %coarse_ref.1, f32[8,256]{1,0:T(8,128)} %constant.4.clone.pos_ref, bf16[256,256]{1,0:T(8,128)(2,1)} %wq_ref.1, bf16[256,256]{1,0:T(8,128)(2,1)} %wk_ref.1, bf16[256,256]{1,0:T(8,128)(2,1)} %wv_ref.1, ...), custom_call_target="tpu_custom_call" | custom-call | tf_op jit(solution)/shard_map/fused/pallas_call | solution.py:306
  68.3 3.1 %copy.12 = bf16[4,4,256,256]{3,2,1,0:T(8,128)(2,1)} copy(bf16[4,4,256,256]{3,2,1,0:T(8,128)(2,1)} %fused.1) | data formatting | bytes 4194304

commit v2 on v1

--- a/solution.py
+++ b/solution.py
@@ -10,7 +10,7 @@
 
 HEADS = 8
 CHUNKS = 4
-HALO = 2
+HALO = 1
 LOG2E = 1.4426950408889634
 MESH = pl.DeviceIdType.MESH
 
@@ -75,15 +75,18 @@
     ref[at * cols : (at + 1) * cols, 2 * width :] = right.astype(jnp.bfloat16)
 
 
-def conv_rows(ref, start, count, cols, weight_ref):
-    pieces = [ref[(start + step) * cols : (start + step + count) * cols, :] for step in range(3)]
-    return jnp.dot(jnp.concatenate(pieces, axis=1), weight_ref[...], preferred_element_type=jnp.float32)
+def conv_rows(ref, start, first, last, cols, weight_ref):
+    pieces = [ref[(start + step) * cols : (start + step + 1) * cols, :] for step in range(first, last)]
+    depth = ref.shape[1]
+    return jnp.dot(
+        jnp.concatenate(pieces, axis=1), weight_ref[first * depth : last * depth, :], preferred_element_type=jnp.float32
+    )
 
 
 def kernel(
     bands, halves, fine_ref, coarse_ref, pos_ref, wq_ref, wk_ref, wv_ref, wo_ref, w1_hbm, w2_hbm, lift_ref, out_ref,
-    mine, other, moved, coarse, x_ref, f_ref, w1_ref, w2_ref, outs,
-    local_sems, fine_send, fine_recv, halo_send, halo_recv, coarse_send, coarse_recv, out_sems,
+    mine, other, moved, coarse, x_ref, f_ref, w1_ref, w2_ref, edges, part_out, part_in,
+    local_sems, fine_send, fine_recv, halo_send, halo_recv, part_send, part_recv, out_sems,
 ):
     own, rows, cols, width = mine.shape
     half = rows // 2
@@ -117,11 +120,11 @@
             src_ref=src, dst_ref=dst, send_sem=send, recv_sem=recv, device_id={"space": place - 1}, device_id_type=MESH
         )
 
-    def coarse_up():
-        return to_after(coarse_ref.at[:, half - 1 : half], coarse.at[:, 0:1], coarse_send.at[0], coarse_recv.at[0])
-
-    def coarse_down():
-        return to_before(coarse_ref.at[:, 0:1], coarse.at[:, half + 1 : half + 2], coarse_send.at[1], coarse_recv.at[1])
+    def part_up(frame):
+        return to_after(part_out.at[0, frame], part_in.at[0, frame], part_send.at[0, frame], part_recv.at[0, frame])
+
+    def part_down(frame):
+        return to_before(part_out.at[1, frame], part_in.at[1, frame], part_send.at[1, frame], part_recv.at[1, frame])
 
     def halo_up(frames, span_at, piece):
         return to_after(
@@ -154,7 +157,7 @@
 
     for chunk in range(CHUNKS):
         mine_copy(chunk).start()
-    own_coarse = pltpu.make_async_copy(coarse_ref, coarse.at[:, 1 : half + 1], local_sems.at[CHUNKS])
+    own_coarse = pltpu.make_async_copy(coarse_ref, coarse, local_sems.at[CHUNKS])
     first_weights = pltpu.make_async_copy(w1_hbm, w1_ref, local_sems.at[CHUNKS + 1])
     second_weights = pltpu.make_async_copy(w2_hbm, w2_ref, local_sems.at[CHUNKS + 2])
 
@@ -176,8 +179,6 @@
     for shift in range(1, halves):
         for chunk in range(CHUNKS):
             fine_copy(shift, chunk).start()
-    pl.when(has_after)(lambda: coarse_up().start())
-    pl.when(has_before)(lambda: coarse_down().start())
     own_coarse.start()
     first_weights.start()
     second_weights.start()
@@ -185,64 +186,73 @@
     @pl.when(jnp.logical_not(has_before))
     def _():
         moved[:, 0:HALO] = jnp.zeros((own, HALO, cols, width), jnp.bfloat16)
+        part_in[0] = jnp.zeros((own, cols, width), jnp.bfloat16)
 
     @pl.when(jnp.logical_not(has_after))
     def _():
         moved[:, rows + HALO :] = jnp.zeros((own, HALO, cols, width), jnp.bfloat16)
+        part_in[1] = jnp.zeros((own, cols, width), jnp.bfloat16)
 
     pos = []
     for shift in range(halves):
         for frame in range(own):
             pos.append(pos_ref[pl.ds(lax.rem(core + shift, halves) * own + frame, 1), :])
 
-    def motion_step(step, carry):
-        chunk, row = step // rows, lax.rem(step, rows)
+    def motion_tile(chunk, row):
         span_at = pl.ds(pl.multiple_of(chunk * span, span), span)
-
-        @pl.when(row == 0)
-        def _():
-            mine_copy(chunk).wait()
-            for shift in range(1, halves):
-                fine_copy(shift, chunk).wait_recv()
-
         here = [mine[frame, row, span_at, :] for frame in range(own)]
         there = [other[frame, row, span_at, :] for frame in range(own * (halves - 1))]
         branch = attention(here, there, pos, wq_ref, wk_ref, wv_ref, wo_ref)
         for frame in range(own):
             moved[frame, row + HALO, span_at, :] = (here[frame].astype(jnp.float32) + branch[frame]).astype(jnp.bfloat16)
 
-        @pl.when((row == rows - 1) & (chunk == 0))
+    def edge_step(step, carry):
+        chunk, edge = step // 2, lax.rem(step, 2)
+        span_at = pl.ds(pl.multiple_of(chunk * span, span), span)
+
+        @pl.when(edge == 0)
+        def _():
+            mine_copy(chunk).wait()
+            for shift in range(1, halves):
+                fine_copy(shift, chunk).wait_recv()
+
+        motion_tile(chunk, edge * (rows - 1))
+
+        @pl.when((edge == 1) & (chunk == 0))
         def _():
             both(pl.ds(0, own), pl.ds(0, span), 0, start, start)
 
-        @pl.when((row == rows - 1) & (chunk > 0))
+        @pl.when((edge == 1) & (chunk > 0))
         def _():
             both(pl.ds(0, early), span_at, chunk, start, start)
 
         return carry
 
-    lax.fori_loop(0, CHUNKS * rows, motion_step, 0)
+    def inner_step(step, carry):
+        motion_tile(step // (rows - 2), 1 + lax.rem(step, rows - 2))
+        return carry
+
+    lax.fori_loop(0, CHUNKS * 2, edge_step, 0)
     rest = pl.ds(span, cols - span)
     for frame in range(early, own):
         both(pl.ds(frame, 1), rest, CHUNKS + frame - early, start, start)
+    lax.fori_loop(0, CHUNKS * (rows - 2), inner_step, 0)
 
     own_coarse.wait()
     first_weights.wait()
     second_weights.wait()
-    pl.when(has_before)(lambda: coarse_up().wait_recv())
-    pl.when(has_after)(lambda: coarse_down().wait_recv())
-
-    @pl.when(jnp.logical_not(has_before))
-    def _():
-        coarse[:, 0] = coarse[:, 1]
-
-    @pl.when(jnp.logical_not(has_after))
-    def _():
-        coarse[:, half + 1] = coarse[:, half]
-
-    def out_copy(frame):
-        slot = lax.rem(frame, 2)
-        return pltpu.make_async_copy(outs.at[slot], out_ref.at[frame], out_sems.at[slot])
+
+    def inner_copy(frame):
+        return pltpu.make_async_copy(
+            mine.at[frame, 1 : rows - 1], out_ref.at[frame, 1 : rows - 1], out_sems.at[0, frame]
+        )
+
+    def edge_copy(frame, side):
+        row = side * (rows - 1)
+        return pltpu.make_async_copy(mine.at[frame, row], out_ref.at[frame, row], out_sems.at[1 + side, frame])
+
+    def lifted(near, far):
+        return jnp.dot(lift_ref[...], jnp.concatenate([near, far], axis=0), preferred_element_type=jnp.float32)
 
     def conv_step(frame, carry):
         @pl.when(frame == 0)
@@ -257,36 +267,58 @@
 
         for r in range(rows + 2 * HALO):
             spread_columns(x_ref, r, jnp.maximum(moved[frame, r].astype(jnp.float32), 0.0), cols)
-        for r in range(rows + 2):
-            first = conv_rows(x_ref, r, 1, cols, w1_ref)
+        for r in range(rows):
+            first = conv_rows(x_ref, r, 0, 3, cols, w1_ref)
             first = jnp.maximum(first, 0.0).astype(jnp.bfloat16).astype(jnp.float32)
+            spread_columns(f_ref, r, first, cols)
+        top, bottom = coarse[frame, 0], coarse[frame, half - 1]
+        none = jnp.zeros_like(top)
+        part = conv_rows(f_ref, rows - 1, 0, 1, cols, w2_ref) + lifted(none, bottom)
+        part_out[0, frame] = part.astype(jnp.bfloat16)
+        part = conv_rows(f_ref, -2, 2, 3, cols, w2_ref) + lifted(none, top)
+        part_out[1, frame] = part.astype(jnp.bfloat16)
+        pl.when(has_after)(lambda: part_up(frame).start())
+        pl.when(has_before)(lambda: part_down(frame).start())
+        for r in range(rows):
+            near = coarse[frame, r // 2]
             if r == 0:
-                first = jnp.where(has_before, first, 0.0)
-            if r == rows + 1:
-                first = jnp.where(has_after, first, 0.0)
-            spread_columns(f_ref, r, first, cols)
-
-        @pl.when(frame >= 2)
-        def _():
-            out_copy(frame - 2).wait()
-
-        for r in range(rows):
-            near = coarse[frame, r // 2 + 1]
-            far = coarse[frame, r // 2] if r % 2 == 0 else coarse[frame, r // 2 + 2]
-            up = jnp.dot(lift_ref[...], jnp.concatenate([near, far], axis=0), preferred_element_type=jnp.float32)
-            second = conv_rows(f_ref, r, 1, cols, w2_ref)
-            outs[lax.rem(frame, 2), r] = (up + moved[frame, r + HALO].astype(jnp.float32) + second).astype(jnp.bfloat16)
-        out_copy(frame).start()
+                far = jnp.where(has_before, none, near)
+            elif r == rows - 1:
+                far = jnp.where(has_after, none, near)
+            else:
+                far = coarse[frame, r // 2 - 1] if r % 2 == 0 else coarse[frame, r // 2 + 1]
+            second = conv_rows(f_ref, r - 1, 1 if r == 0 else 0, 2 if r == rows - 1 else 3, cols, w2_ref)
+            joined = lifted(near, far) + moved[frame, r + HALO].astype(jnp.float32) + second
+            if r == 0:
+                edges[frame, 0] = joined
+            elif r == rows - 1:
+                edges[frame, 1] = joined
+            else:
+                mine[frame, r] = joined.astype(jnp.bfloat16)
+        inner_copy(frame).start()
         return carry
 
     lax.fori_loop(0, own, conv_step, 0)
-    for frame in range(max(own - 2, 0), own):
-        out_copy(frame).wait()
+
+    def join_step(frame, carry):
+        pl.when(has_before)(lambda: part_up(frame).wait_recv())
+        mine[frame, 0] = (edges[frame, 0] + part_in[0, frame].astype(jnp.float32)).astype(jnp.bfloat16)
+        edge_copy(frame, 0).start()
+        pl.when(has_after)(lambda: part_down(frame).wait_recv())
+        mine[frame, rows - 1] = (edges[frame, 1] + part_in[1, frame].astype(jnp.float32)).astype(jnp.bfloat16)
+        edge_copy(frame, 1).start()
+        return carry
+
+    lax.fori_loop(0, own, join_step, 0)
+    for frame in range(own):
+        inner_copy(frame).wait()
+        edge_copy(frame, 0).wait()
+        edge_copy(frame, 1).wait()
+        pl.when(has_after)(lambda: part_up(frame).wait_send())
+        pl.when(has_before)(lambda: part_down(frame).wait_send())
     for shift in range(1, halves):
         for chunk in range(CHUNKS):
             fine_copy(shift, chunk).wait_send()
-    pl.when(has_after)(lambda: coarse_up().wait_send())
-    pl.when(has_before)(lambda: coarse_down().wait_send())
     both(pl.ds(0, own), pl.ds(0, span), 0, wait_send, wait_send)
     for chunk in range(1, CHUNKS):
         both(pl.ds(0, early), pl.ds(chunk * span, span), chunk, wait_send, wait_send)
@@ -312,20 +344,22 @@
             pltpu.VMEM((own, rows, cols, width), bf16),
             pltpu.VMEM((far, rows, cols, width), bf16),
             pltpu.VMEM((own, rows + 2 * HALO, cols, width), bf16),
-            pltpu.VMEM((own, half + 2, small, width), bf16),
-            pltpu.VMEM(((rows + 4) * cols, 3 * width), bf16),
-            pltpu.VMEM(((rows + 2) * cols, 3 * width), bf16),
+            pltpu.VMEM((own, half, small, width), bf16),
+            pltpu.VMEM(((rows + 2 * HALO) * cols, 3 * width), bf16),
+            pltpu.VMEM((rows * cols, 3 * width), bf16),
             pltpu.VMEM((9 * width, width), bf16),
             pltpu.VMEM((9 * width, width), bf16),
-            pltpu.VMEM((2, rows, cols, width), bf16),
+            pltpu.VMEM((own, 2, cols, width), jnp.float32),
+            pltpu.VMEM((2, own, cols, width), bf16),
+            pltpu.VMEM((2, own, cols, width), bf16),
             pltpu.SemaphoreType.DMA((CHUNKS + 3,)),
             pltpu.SemaphoreType.DMA((halves - 1, CHUNKS)),
             pltpu.SemaphoreType.DMA((halves - 1, CHUNKS)),
             pltpu.SemaphoreType.DMA((2, pieces)),
             pltpu.SemaphoreType.DMA((2, pieces)),
-            pltpu.SemaphoreType.DMA((2,)),
-            pltpu.SemaphoreType.DMA((2,)),
-            pltpu.SemaphoreType.DMA((2,)),
+            pltpu.SemaphoreType.DMA((2, own)),
+            pltpu.SemaphoreType.DMA((2, own)),
+            pltpu.SemaphoreType.DMA((3, own)),
         ],
         compiler_params=pltpu.CompilerParams(
             collective_id=0, has_side_effects=True, vmem_limit_bytes=62 * 1024 * 1024

time: 72.5 us -> 60.5 us (0.83)
  the two profiles are of different devices: /device:TPU:21 before, /device:TPU:0 now
where the time goes in v2:
time: 60.5 us; the launch traced here: 60.3 us
  Pallas kernels  57.2 us (95%)
  local copies, waits for them, and re-layouts  3.1 us (5%)
    pallas_call x1, Pallas kernels, local(): pl.pallas_call(functools.partial(kernel, bands, halves), in_specs=[any_sp...  57.2 us
    unnamed x1, local copies, waits for them, and re-layouts  3.1 us

profile of v2, /device:TPU:0, one launch (start us, length us, event | category | flops | bytes accessed | tf_op | source)
XLA Modules:
  0.0 60.3 jit_solution(18049216909069987143)
XLA Ops:
  0.0 57.2 %fused.1 = bf16[4,4,256,256]{3,2,1,0:T(8,128)(2,1)} custom-call(bf16[4,4,256,256]{3,2,1,0:T(8,128)(2,1)} %fine_ref.1, bf16[4,2,128,256]{3,2,1,0:T(8,128)(2,1)} %coarse_ref.1, f32[8,256]{1,0:T(8,128)} %constant.4.clone.pos_ref, bf16[256,256]{1,0:T(8,128)(2,1)} %wq_ref.1, bf16[256,256]{1,0:T(8,128)(2,1)} %wk_ref.1, bf16[256,256]{1,0:T(8,128)(2,1)} %wv_ref.1, ...), custom_call_target="tpu_custom_call" | custom-call | tf_op jit(solution)/shard_map/fused/pallas_call | solution.py:338
  57.2 3.1 %copy.12 = bf16[4,4,256,256]{3,2,1,0:T(8,128)(2,1)} copy(bf16[4,4,256,256]{3,2,1,0:T(8,128)(2,1)} %fused.1) | data formatting | bytes 4194304
